TPU v7x, 32 devices: a whole 2x2x4 slice. The times are simulated.
32 devices in a mesh: owner: 4 (over y, x), rows: 8 (over z, core).
Axes of the slice: x: 2, y: 2, z: 4, core: 2. Of those that a mesh axis runs over, the one named last changes fastest.
Arguments:
- train_gate: float32 [64, 2048, 1024], P('owner', 'rows'), may hold values from -0.1875 to 0.1875
- train_up: float32 [64, 2048, 1024], P('owner', 'rows'), may hold values from -0.1875 to 0.1875
- train_down: float32 [64, 1024, 2048], P('owner', None, 'rows'), may hold values from -0.25 to 0.25
- router_weight: float32 [2048, 64], P('rows', 'owner'), may hold values from -0.125 to 0.125
- router_gain: float32 [2048], P('rows'), may hold values from 0.25 to 1.75
Outputs:
- ready_gate: bfloat16 [64, 2048, 1024], P('owner', None, 'rows')
- ready_up: bfloat16 [64, 2048, 1024], P('owner', None, 'rows')
- ready_down: bfloat16 [64, 1024, 2048], P('owner', 'rows')
- scale_gate: float32 [64, 1024], P('owner', 'rows')
- scale_up: float32 [64, 1024], P('owner', 'rows')
- scale_down: float32 [64, 1024], P('owner', 'rows')
- serve_router: bfloat16 [2048, 64], replicated
All inputs are finite; a program needn't handle non-finite values. Where the computation divides by a largest or mean magnitude, that divisor is 1e-20 or more.
Results may differ from a plain program's by a relative error of at most 0.0013.
Values may be sent and summed in bfloat16 or wider, within the bound.
A program may use at most 192 MiB of HBM per device.

v0:
```python
import jax
import jax.numpy as jnp
from jax import lax
from jax.sharding import PartitionSpec as P

D_MODEL = 2048


def local(train_gate, train_up, train_down, router_weight, router_gain):
    total_gate, total_up, total_down = lax.psum(
        (
            jnp.sum(jnp.abs(train_gate), axis=1),
            jnp.sum(jnp.abs(train_up), axis=1),
            jnp.sum(jnp.abs(train_down), axis=2),
        ),
        "rows",
    )
    scale_gate = total_gate / D_MODEL
    scale_up = total_up / D_MODEL
    scale_down = total_down / D_MODEL
    narrow_gate, narrow_up, narrow_down = (
        (train_gate / jnp.expand_dims(scale_gate, 1)).astype(jnp.bfloat16),
        (train_up / jnp.expand_dims(scale_up, 1)).astype(jnp.bfloat16),
        (train_down / jnp.expand_dims(scale_down, 2)).astype(jnp.bfloat16),
    )
    ready_gate, ready_up = (
        lax.all_to_all(narrow_gate, "rows", split_axis=2, concat_axis=1, tiled=True),
        lax.all_to_all(narrow_up, "rows", split_axis=2, concat_axis=1, tiled=True),
    )
    ready_down = lax.all_to_all(narrow_down, "rows", split_axis=1, concat_axis=2, tiled=True)
    scale_gate = lax.dynamic_slice_in_dim(
        scale_gate, lax.axis_index("rows") * ready_gate.shape[2], ready_gate.shape[2], axis=1
    )
    scale_up = lax.dynamic_slice_in_dim(
        scale_up, lax.axis_index("rows") * ready_up.shape[2], ready_up.shape[2], axis=1
    )
    scale_down = lax.dynamic_slice_in_dim(
        scale_down, lax.axis_index("rows") * ready_down.shape[1], ready_down.shape[1], axis=1
    )
    part_router = (router_weight * router_gain[:, None]).astype(jnp.bfloat16)
    row_router = lax.all_gather(part_router, "rows", axis=0, tiled=True)
    serve_router = lax.all_gather(row_router, "owner", axis=1, tiled=True)
    return (ready_gate, ready_up, ready_down, scale_gate, scale_up, scale_down, serve_router)


def solution(mesh):
    return jax.shard_map(
        local,
        mesh=mesh,
        in_specs=(
            P("owner", "rows", None),
            P("owner", "rows", None),
            P("owner", None, "rows"),
            P("rows", "owner"),
            P("rows"),
        ),
        out_specs=(
            P("owner", None, "rows"),
            P("owner", None, "rows"),
            P("owner", "rows", None),
            P("owner", "rows"),
            P("owner", "rows"),
            P("owner", "rows"),
            P(),
        ),
        check_vma=False,
    )
```

profile of v0, /device:TPU:0, one launch (start us, length us, event | category | flops | bytes accessed | tf_op | source)
XLA Modules:
  0.0 737.8 jit_solution(7608499507201470121)
XLA Ops:
  7.2 0.0 all-reduce.3.cloned.1.call-start
  7.2 8.6 %abs_reduce_fusion = f32[16,1024]{1,0:T(8,128)} fusion(f32[16,1024,256]{2,1,0:T(8,128)} %param.7), kind=kLoop, calls=%fused_computation.2 | loop fusion | flops 8372224 | bytes 16842752 | tf_op jit(solution)/shard_map/reduce_sum | solution.py:14
  15.8 12.6 %abs_reduce_fusion.1 = (f32[16,1024]{1,0:T(8,128)}, f32[16,1024]{1,0:T(8,128)}) fusion(f32[16,256,1024]{2,1,0:T(8,128)} %param.6, f32[16,256,1024]{2,1,0:T(8,128)} %param.5), kind=kLoop, calls=%fused_computation.4 | loop fusion | flops 16744448 | bytes 33685504 | tf_op jit(solution)/shard_map/reduce_sum | solution.py:13
  28.4 0.0 all-reduce.3.cloned.1.call-update
  28.4 17.6 %copy.19 = f32[16,256,1024]{1,0,2:T(8,128)} copy(f32[16,256,1024]{2,1,0:T(8,128)} %param.6) | data formatting | bytes 33554432 | tf_op args[1]
  46.1 40.7 %all-reduce.3.cloned.1.call-done = (f32[16,1024]{1,0:T(8,128)}, f32[16,1024]{1,0:T(8,128)}, f32[16,1024]{1,0:T(8,128)}) async-done(((f32[16,1024]{1,0:T(8,128)}, f32[16,1024]{1,0:T(8,128)}, f32[16,1024]{1,0:T(8,128)}), (f32[16,1024]{1,0:T(8,128)}, f32[16,1024]{1,0:T(8,128)}, f32[16,1024]{1,0:T(8,128)})) %all-reduce.3.cloned.1.call-update) | async-done | bytes 196624 | tf_op jit(solution)/shard_map/psum | solution.py:10
  86.8 0.8 broadcast_multiply_fusion.1
  87.6 0.2 copy.18
  87.8 9.6 %divide_convert_fusion = bf16[16,256,1024]{1,0,2:T(8,128)(2,1)} fusion(f32[16,256,1024]{1,0,2:T(8,128)} %copy.19, f32[16,1024]{0,1:T(8,128)S(1)} %copy.18), kind=kLoop, calls=%fused_computation.3 | loop fusion | flops 8388608 | bytes 25231360 | tf_op jit(solution)/shard_map/convert_element_type | solution.py:23
  97.5 4.9 all-to-all-start.1
  102.4 0.0 copy-start.1
  102.4 17.6 %copy.16 = f32[16,256,1024]{1,0,2:T(8,128)} copy(f32[16,256,1024]{2,1,0:T(8,128)} %param.5) | data formatting | bytes 33554432 | tf_op args[0]
  120.0 0.0 copy-done.1
  120.0 0.2 copy.15
  120.2 0.0 copy-start
  120.3 9.7 %divide_convert_fusion.1 = bf16[16,256,1024]{1,0,2:T(8,128)(2,1)} fusion(f32[16,256,1024]{1,0,2:T(8,128)} %copy.16, f32[16,1024]{0,1:T(8,128)S(1)} %copy.15), kind=kLoop, calls=%fused_computation.5 | loop fusion | flops 8388608 | bytes 25231360 | tf_op jit(solution)/shard_map/convert_element_type | solution.py:22
  129.9 156.3 %all-to-all-done.1 = bf16[16,256,1024]{1,0,2:T(8,128)(2,1)} async-done(((bf16[16,256,1024]{1,0,2:T(8,128)(2,1)}), bf16[16,256,1024]{1,0,2:T(8,128)(2,1)}, u32[]{:S(2)}, u32[]{:S(2)}) %all-to-all-start.1) | async-done | bytes 8388640 | tf_op jit(solution)/shard_map/all_to_all | solution.py:28
  286.3 4.9 all-to-all-start
  291.2 0.0 copy-done
  291.2 0.2 copy.21
  291.4 0.0 copy-start.2
  291.4 0.0 copy-start.3
  291.5 16.6 %fusion = bf16[16,1024,256]{2,0,1:T(8,128)(2,1)} fusion(f32[16,1024,256]{2,1,0:T(8,128)} %param.7, f32[16,1024]{0,1:T(8,128)S(1)} %copy.21), kind=kLoop, calls=%fused_computation.1 | loop fusion | flops 8388608 | bytes 25231360 | tf_op jit(solution)/shard_map/convert_element_type | solution.py:24
  308.1 167.0 %all-to-all-done = bf16[16,256,1024]{1,0,2:T(8,128)(2,1)} async-done(((bf16[16,256,1024]{1,0,2:T(8,128)(2,1)}), bf16[16,256,1024]{1,0,2:T(8,128)(2,1)}, u32[]{:S(2)}, u32[]{:S(2)}) %all-to-all-start) | async-done | bytes 8388640 | tf_op jit(solution)/shard_map/all_to_all | solution.py:27
  475.1 5.0 all-to-all-start.2
  480.1 0.0 copy-done.2
  480.1 0.0 copy-done.3
  480.1 189.9 %all_gather.6 = bf16[2048,16]{0,1:T(8,128)(2,1)S(1)} all-gather(bf16[256,16]{0,1:T(8,128)(2,1)S(1)} %multiply_convert_fusion), channel_id=1, replica_groups=mesh['owner'=4,'rows'=8] {'rows'}, dimensions={0}, use_global_device_ids=true | all-gather | bytes 73728 | tf_op jit(solution)/shard_map/all_gather | solution.py:41
  670.0 9.1 %all_gather.7 = bf16[2048,64]{0,1:T(8,128)(2,1)S(1)} all-gather(bf16[2048,16]{0,1:T(8,128)(2,1)S(1)} %all_gather.6), channel_id=1, replica_groups=mesh['owner'=4,'rows'=8] {'owner'}, dimensions={1}, use_global_device_ids=true | all-gather | bytes 327680 | tf_op jit(solution)/shard_map/all_gather | solution.py:42
  679.1 0.6 constant_dynamic-slice_fusion
  679.7 0.6 constant_dynamic-slice_fusion.1
  680.3 0.6 constant_dynamic-slice_fusion.2
  680.9 12.3 %copy.20 = bf16[16,8,256,128]{3,2,1,0:T(8,128)(2,1)} copy(bf16[16,8,256,128]{2,0,3,1:T(8,128)(2,1)} %bitcast.4) | data formatting | bytes 16777216 | tf_op jit(solution)/shard_map/all_to_all | solution.py:28
  693.2 12.3 %copy.17 = bf16[16,8,256,128]{3,2,1,0:T(8,128)(2,1)} copy(bf16[16,8,256,128]{2,0,3,1:T(8,128)(2,1)} %bitcast.1) | data formatting | bytes 16777216 | tf_op jit(solution)/shard_map/all_to_all | solution.py:27
  705.5 0.0 all-to-all-done.2
  705.5 11.4 %copy.23 = bf16[16,128,8,256]{3,2,1,0:T(8,128)(2,1)} copy(bf16[16,128,8,256]{3,0,1,2:T(8,128)(2,1)} %bitcast.7) | data formatting | bytes 16777216 | tf_op jit(solution)/shard_map/all_to_all | solution.py:30
  716.9 13.4 %all_to_all.50 = bf16[16,128,2048]{2,1,0:T(8,128)(2,1)} reshape(bf16[16,128,8,256]{3,2,1,0:T(8,128)(2,1)} %copy.23) | data formatting | bytes 16777216 | tf_op jit(solution)/shard_map/all_to_all | solution.py:30
  730.3 0.7 copy.31
  (3 shorter events, 0.0 us)
Async XLA Ops:
  7.2 79.6 %all-reduce.3.cloned.1.call-start = ((), (), s32[]{:S(2)}) async-start(), calls=%async_computation.3 | async-start | bytes 393216 | tf_op jit(solution)/shard_map/psum | solution.py:10
  97.5 188.8 %all-to-all-start.1 = ((bf16[16,256,1024]{1,0,2:T(8,128)(2,1)}), bf16[16,256,1024]{1,0,2:T(8,128)(2,1)}, u32[]{:S(2)}, u32[]{:S(2)}) async-start(bf16[16,256,1024]{1,0,2:T(8,128)(2,1)} %divide_convert_fusion), calls=%async_computation.1 | async-start | bytes 16777216 | tf_op jit(solution)/shard_map/all_to_all | solution.py:28
  102.4 17.6 %copy-start.1 = (f32[16,1024]{1,0:T(8,128)S(1)}, f32[16,1024]{1,0:T(8,128)}, u32[]{:S(2)}) copy-start(f32[16,1024]{1,0:T(8,128)} %get-tuple-element.7) | copy-start | bytes 196612
  120.2 171.0 %copy-start = (f32[16,1024]{1,0:T(8,128)S(1)}, f32[16,1024]{1,0:T(8,128)}, u32[]{:S(2)}) copy-start(f32[16,1024]{1,0:T(8,128)} %get-tuple-element.9) | copy-start | bytes 196612
  286.3 188.8 %all-to-all-start = ((bf16[16,256,1024]{1,0,2:T(8,128)(2,1)}), bf16[16,256,1024]{1,0,2:T(8,128)(2,1)}, u32[]{:S(2)}, u32[]{:S(2)}) async-start(bf16[16,256,1024]{1,0,2:T(8,128)(2,1)} %divide_convert_fusion.1), calls=%async_computation | async-start | bytes 16777216 | tf_op jit(solution)/shard_map/all_to_all | solution.py:27
  291.4 188.7 %copy-start.2 = (f32[256,16]{0,1:T(8,128)S(1)}, f32[256,16]{0,1:T(8,128)}, u32[]{:S(2)}) copy-start(f32[256,16]{0,1:T(8,128)} %param.8) | copy-start | bytes 49156
  291.4 188.7 %copy-start.3 = (f32[256]{0:T(256)S(1)}, f32[256]{0:T(256)}, u32[]{:S(2)}) copy-start(f32[256]{0:T(256)} %param.9) | copy-start | bytes 3076
  475.1 230.4 %all-to-all-start.2 = ((bf16[16,1024,256]{2,0,1:T(8,128)(2,1)}), bf16[16,1024,256]{2,0,1:T(8,128)(2,1)}, u32[]{:S(2)}, u32[]{:S(2)}) async-start(bf16[16,1024,256]{2,0,1:T(8,128)(2,1)} %fusion), calls=%async_computation.2 | async-start | bytes 16777216 | tf_op jit(solution)/shard_map/all_to_all | solution.py:30
Sparse Core Ops, SparseCore 0:
  28.6 58.1 all-reduce.2
where the time goes:
time: 740 us; the launch traced here: 738 us
  waiting for transfers between devices  364 us (49%)
  blocking collectives  199 us (27%)
  local copies, waits for them, and re-layouts  87.7 us (12%)
  other arithmetic  58 us (8%)
  starting transfers between devices  14.9 us (2%)
  between operations  14.2 us (2%)
    all_gather x1, blocking collectives, local(): row_router = lax.all_gather(part_router, 'rows', axis=0, tiled=True)  190 us
    all_to_all x1, waiting for transfers between devices, local(): lax.all_to_all(narrow_gate, 'rows', split_axis=2, concat_axis=1, tiled=True)  167 us
    all_to_all x1, waiting for transfers between devices, local(): lax.all_to_all(narrow_up, 'rows', split_axis=2, concat_axis=1, tiled=True)  156 us
    psum x1, waiting for transfers between devices, local(): lax.psum((jnp.sum(jnp.abs(train_gate), axis=1), jnp.sum(jnp.abs(train_up)...  40.7 us
    unnamed x11, local copies, waits for them, and re-layouts  36 us
    all_to_all x2, local copies, waits for them, and re-layouts, local(): lax.all_to_all(narrow_down, 'rows', split_axis=1, concat_axis=2, tiled=True)  24.8 us
    convert_element_type x1, other arithmetic, local(): (train_down / jnp.expand_dims(scale_down, 2)).astype(jnp.bfloat16)  16.6 us
  transfers between devices with their start and end apart: 4, of which 3 were waited for; matrix products, arithmetic and copies ran while one was open for 12% of the time, Pallas kernels for 0%

commit v1 on v0

--- a/solution.py
+++ b/solution.py
@@ -2,6 +2,7 @@
 import jax.numpy as jnp
 from jax import lax
 from jax.sharding import PartitionSpec as P
+from jax.lax import all_to_all, psum
 
 D_MODEL = 2048
 
@@ -39,7 +40,10 @@
     )
     part_router = (router_weight * router_gain[:, None]).astype(jnp.bfloat16)
     row_router = lax.all_gather(part_router, "rows", axis=0, tiled=True)
-    serve_router = lax.all_gather(row_router, "owner", axis=1, tiled=True)
+    parts_seen = []
+    for _ in range(psum(1, "owner")):
+        parts_seen.append(row_router)
+    serve_router = jnp.concatenate(all_to_all(jnp.stack(parts_seen), "owner", 0, 0), axis=1)
     return (ready_gate, ready_up, ready_down, scale_gate, scale_up, scale_down, serve_router)
 
 

time: 740 us -> 698 us (0.943)
  blocking collectives: 199 us -> 15.7 us
  waiting for transfers between devices: 364 us -> 501 us
    all_gather x1, blocking collectives: 190 us -> 15.7 us  [local(): row_router = lax.all_gather(part_router, 'rows', axis=0, tiled=True)]
    all_to_all x1, waiting for transfers between devices: 0.01 us -> 157 us  [local(): lax.all_to_all(narrow_down, 'rows', split_axis=1, concat_axis=2, tiled=True)]
    psum x1, waiting for transfers between devices: 40.7 us -> 20.6 us  [local(): lax.psum((jnp.sum(jnp.abs(train_gate), axis=1), jnp.sum(jnp.abs(train_up)...]
    all_gather x1 -> x0, blocking collectives: 9.11 us -> none  [local(): serve_router = lax.all_gather(row_router, 'owner', axis=1, tiled=True)]
  transfers between devices with their start and end apart: 4 -> 5, of which waited for: 3 -> 4; matrix products, arithmetic and copies ran while one was open for 12% -> 14% of each run, Pallas kernels for 0% -> 0%
where the time goes in v1:
time: 698 us; the launch traced here: 696 us
  waiting for transfers between devices  501 us (72%)
  local copies, waits for them, and re-layouts  88.4 us (13%)
  other arithmetic  58 us (8%)
  starting transfers between devices  18.9 us (3%)
  blocking collectives  15.7 us (2%)
  between operations  14.2 us (2%)
    all_to_all x1, waiting for transfers between devices, local(): lax.all_to_all(narrow_gate, 'rows', split_axis=2, concat_axis=1, tiled=True)  167 us
    all_to_all x1, waiting for transfers between devices, local(): lax.all_to_all(narrow_down, 'rows', split_axis=1, concat_axis=2, tiled=True)  157 us
    all_to_all x1, waiting for transfers between devices, local(): lax.all_to_all(narrow_up, 'rows', split_axis=2, concat_axis=1, tiled=True)  156 us
    unnamed x11, local copies, waits for them, and re-layouts  35.9 us
    all_to_all x2, local copies, waits for them, and re-layouts, local(): lax.all_to_all(narrow_down, 'rows', split_axis=1, concat_axis=2, tiled=True)  24.8 us
    psum x1, waiting for transfers between devices, local(): lax.psum((jnp.sum(jnp.abs(train_gate), axis=1), jnp.sum(jnp.abs(train_up)...  20.6 us
    convert_element_type x1, other arithmetic, local(): (train_down / jnp.expand_dims(scale_down, 2)).astype(jnp.bfloat16)  16.6 us
    all_gather x1, blocking collectives, local(): row_router = lax.all_gather(part_router, 'rows', axis=0, tiled=True)  15.7 us
  transfers between devices with their start and end apart: 5, of which 4 were waited for; matrix products, arithmetic and copies ran while one was open for 14% of the time, Pallas kernels for 0%

profile of v1, /device:TPU:0, one launch (start us, length us, event | category | flops | bytes accessed | tf_op | source)
XLA Modules:
  0.0 696.4 jit_solution(16060710128545141370)
XLA Ops:
  7.2 0.0 all-reduce.3.cloned.1.call-start
  7.2 8.6 %abs_reduce_fusion = f32[16,1024]{1,0:T(8,128)} fusion(f32[16,1024,256]{2,1,0:T(8,128)} %param.7), kind=kLoop, calls=%fused_computation.2 | loop fusion | flops 8372224 | bytes 16842752 | tf_op jit(solution)/shard_map/reduce_sum | solution.py:15
  15.8 0.0 copy-start.2
  15.8 0.0 copy-start.3
  15.9 12.6 %abs_reduce_fusion.1 = (f32[16,1024]{1,0:T(8,128)}, f32[16,1024]{1,0:T(8,128)}) fusion(f32[16,256,1024]{2,1,0:T(8,128)} %param.6, f32[16,256,1024]{2,1,0:T(8,128)} %param.5), kind=kLoop, calls=%fused_computation.4 | loop fusion | flops 16744448 | bytes 33685504 | tf_op jit(solution)/shard_map/reduce_sum | solution.py:14
  28.4 0.0 all-reduce.3.cloned.1.call-update
  28.5 0.0 copy-done.2
  28.5 0.0 copy-done.3
  28.5 15.7 %all_gather.3 = bf16[2048,16]{0,1:T(8,128)(2,1)S(1)} all-gather(bf16[256,16]{0,1:T(8,128)(2,1)S(1)} %multiply_convert_fusion), channel_id=1, replica_groups=mesh['owner'=4,'rows'=8] {'rows'}, dimensions={0}, use_global_device_ids=true | all-gather | bytes 73728 | tf_op jit(solution)/shard_map/all_gather | solution.py:42
  44.2 0.7 stack.2
  44.9 3.7 all-to-all-start.3
  48.6 17.6 %copy.19 = f32[16,256,1024]{1,0,2:T(8,128)} copy(f32[16,256,1024]{2,1,0:T(8,128)} %param.6) | data formatting | bytes 33554432 | tf_op args[1]
  66.2 20.6 %all-reduce.3.cloned.1.call-done = (f32[16,1024]{1,0:T(8,128)}, f32[16,1024]{1,0:T(8,128)}, f32[16,1024]{1,0:T(8,128)}) async-done(((f32[16,1024]{1,0:T(8,128)}, f32[16,1024]{1,0:T(8,128)}, f32[16,1024]{1,0:T(8,128)}), (f32[16,1024]{1,0:T(8,128)}, f32[16,1024]{1,0:T(8,128)}, f32[16,1024]{1,0:T(8,128)})) %all-reduce.3.cloned.1.call-update) | async-done | bytes 196624 | tf_op jit(solution)/shard_map/psum | solution.py:11
  86.8 0.8 broadcast_multiply_fusion.1
  87.6 0.2 copy.18
  87.8 9.6 %divide_convert_fusion = bf16[16,256,1024]{1,0,2:T(8,128)(2,1)} fusion(f32[16,256,1024]{1,0,2:T(8,128)} %copy.19, f32[16,1024]{0,1:T(8,128)S(1)} %copy.18), kind=kLoop, calls=%fused_computation.3 | loop fusion | flops 8388608 | bytes 25231360 | tf_op jit(solution)/shard_map/convert_element_type | solution.py:24
  97.5 0.0 all-to-all-done.3
  97.5 5.0 all-to-all-start.1
  102.4 0.0 copy-start.1
  102.4 17.6 %copy.16 = f32[16,256,1024]{1,0,2:T(8,128)} copy(f32[16,256,1024]{2,1,0:T(8,128)} %param.5) | data formatting | bytes 33554432 | tf_op args[0]
  120.1 0.0 copy-done.1
  120.1 0.2 copy.15
  120.3 0.0 copy-start
  120.3 9.7 %divide_convert_fusion.1 = bf16[16,256,1024]{1,0,2:T(8,128)(2,1)} fusion(f32[16,256,1024]{1,0,2:T(8,128)} %copy.16, f32[16,1024]{0,1:T(8,128)S(1)} %copy.15), kind=kLoop, calls=%fused_computation.5 | loop fusion | flops 8388608 | bytes 25231360 | tf_op jit(solution)/shard_map/convert_element_type | solution.py:23
  130.0 156.3 %all-to-all-done.1 = bf16[16,256,1024]{1,0,2:T(8,128)(2,1)} async-done(((bf16[16,256,1024]{1,0,2:T(8,128)(2,1)}), bf16[16,256,1024]{1,0,2:T(8,128)(2,1)}, u32[]{:S(2)}, u32[]{:S(2)}) %all-to-all-start.1) | async-done | bytes 8388640 | tf_op jit(solution)/shard_map/all_to_all | solution.py:29
  286.3 4.9 all-to-all-start
  291.3 0.0 copy-done
  291.3 0.2 copy.21
  291.5 16.6 %fusion = bf16[16,1024,256]{2,0,1:T(8,128)(2,1)} fusion(f32[16,1024,256]{2,1,0:T(8,128)} %param.7, f32[16,1024]{0,1:T(8,128)S(1)} %copy.21), kind=kLoop, calls=%fused_computation.1 | loop fusion | flops 8388608 | bytes 25231360 | tf_op jit(solution)/shard_map/convert_element_type | solution.py:25
  308.1 167.0 %all-to-all-done = bf16[16,256,1024]{1,0,2:T(8,128)(2,1)} async-done(((bf16[16,256,1024]{1,0,2:T(8,128)(2,1)}), bf16[16,256,1024]{1,0,2:T(8,128)(2,1)}, u32[]{:S(2)}, u32[]{:S(2)}) %all-to-all-start) | async-done | bytes 8388640 | tf_op jit(solution)/shard_map/all_to_all | solution.py:28
  475.1 5.2 all-to-all-start.2
  480.3 0.6 constant_dynamic-slice_fusion
  480.9 0.6 constant_dynamic-slice_fusion.1
  481.5 0.6 constant_dynamic-slice_fusion.2
  482.1 12.3 %copy.20 = bf16[16,8,256,128]{3,2,1,0:T(8,128)(2,1)} copy(bf16[16,8,256,128]{2,0,3,1:T(8,128)(2,1)} %bitcast.4) | data formatting | bytes 16777216 | tf_op jit(solution)/shard_map/all_to_all | solution.py:29
  494.4 12.3 %copy.17 = bf16[16,8,256,128]{3,2,1,0:T(8,128)(2,1)} copy(bf16[16,8,256,128]{2,0,3,1:T(8,128)(2,1)} %bitcast.1) | data formatting | bytes 16777216 | tf_op jit(solution)/shard_map/all_to_all | solution.py:28
  506.7 157.3 %all-to-all-done.2 = bf16[16,1024,256]{2,0,1:T(8,128)(2,1)} async-done(((bf16[16,1024,256]{2,0,1:T(8,128)(2,1)}), bf16[16,1024,256]{2,0,1:T(8,128)(2,1)}, u32[]{:S(2)}, u32[]{:S(2)}) %all-to-all-start.2) | async-done | bytes 8388640 | tf_op jit(solution)/shard_map/all_to_all | solution.py:31
  664.0 11.4 %copy.23 = bf16[16,128,8,256]{3,2,1,0:T(8,128)(2,1)} copy(bf16[16,128,8,256]{3,0,1,2:T(8,128)(2,1)} %bitcast.7) | data formatting | bytes 16777216 | tf_op jit(solution)/shard_map/all_to_all | solution.py:31
  675.4 13.4 %all_to_all.53 = bf16[16,128,2048]{2,1,0:T(8,128)(2,1)} reshape(bf16[16,128,8,256]{3,2,1,0:T(8,128)(2,1)} %copy.23) | data formatting | bytes 16777216 | tf_op jit(solution)/shard_map/all_to_all | solution.py:31
  688.8 0.7 copy.31
  (3 shorter events, 0.0 us)
Async XLA Ops:
  7.2 79.6 %all-reduce.3.cloned.1.call-start = ((), (), s32[]{:S(2)}) async-start(), calls=%async_computation.4 | async-start | bytes 393216 | tf_op jit(solution)/shard_map/psum | solution.py:11
  15.8 12.6 %copy-start.2 = (f32[256,16]{0,1:T(8,128)S(1)}, f32[256,16]{0,1:T(8,128)}, u32[]{:S(2)}) copy-start(f32[256,16]{0,1:T(8,128)} %param.8) | copy-start | bytes 49156
  15.8 12.6 %copy-start.3 = (f32[256]{0:T(256)S(1)}, f32[256]{0:T(256)}, u32[]{:S(2)}) copy-start(f32[256]{0:T(256)} %param.9) | copy-start | bytes 3076
  44.9 52.6 %all-to-all-start.3 = ((bf16[4,2048,16]{1,2,0:T(8,128)(2,1)}), bf16[4,2048,16]{1,2,0:T(8,128)(2,1)S(1)}, u32[]{:S(2)}, u32[]{:S(2)}) async-start(bf16[4,2048,16]{1,2,0:T(8,128)(2,1)} %stack.2), calls=%async_computation.3 | async-start | bytes 524288 | tf_op jit(solution)/shard_map/all_to_all | solution.py:46
  97.5 188.8 %all-to-all-start.1 = ((bf16[16,256,1024]{1,0,2:T(8,128)(2,1)}), bf16[16,256,1024]{1,0,2:T(8,128)(2,1)}, u32[]{:S(2)}, u32[]{:S(2)}) async-start(bf16[16,256,1024]{1,0,2:T(8,128)(2,1)} %divide_convert_fusion), calls=%async_computation.1 | async-start | bytes 16777216 | tf_op jit(solution)/shard_map/all_to_all | solution.py:29
  102.4 17.6 %copy-start.1 = (f32[16,1024]{1,0:T(8,128)S(1)}, f32[16,1024]{1,0:T(8,128)}, u32[]{:S(2)}) copy-start(f32[16,1024]{1,0:T(8,128)} %get-tuple-element.7) | copy-start | bytes 196612
  120.3 171.0 %copy-start = (f32[16,1024]{1,0:T(8,128)S(1)}, f32[16,1024]{1,0:T(8,128)}, u32[]{:S(2)}) copy-start(f32[16,1024]{1,0:T(8,128)} %get-tuple-element.9) | copy-start | bytes 196612
  286.3 188.8 %all-to-all-start = ((bf16[16,256,1024]{1,0,2:T(8,128)(2,1)}), bf16[16,256,1024]{1,0,2:T(8,128)(2,1)}, u32[]{:S(2)}, u32[]{:S(2)}) async-start(bf16[16,256,1024]{1,0,2:T(8,128)(2,1)} %divide_convert_fusion.1), calls=%async_computation | async-start | bytes 16777216 | tf_op jit(solution)/shard_map/all_to_all | solution.py:28
  475.1 188.9 %all-to-all-start.2 = ((bf16[16,1024,256]{2,0,1:T(8,128)(2,1)}), bf16[16,1024,256]{2,0,1:T(8,128)(2,1)}, u32[]{:S(2)}, u32[]{:S(2)}) async-start(bf16[16,1024,256]{2,0,1:T(8,128)(2,1)} %fusion), calls=%async_computation.2 | async-start | bytes 16777216 | tf_op jit(solution)/shard_map/all_to_all | solution.py:31
Sparse Core Ops, SparseCore 0:
  28.6 58.1 all-reduce.2
